TPU v7x, 32 devices: a whole 2x2x4 slice. The times are simulated.
32 devices in a mesh: grp: 4 (over z), kv: 4 (over y, x), tp: 2 (over core).
Axes of the slice: x: 2, y: 2, z: 4, core: 2. Of those that a mesh axis runs over, the one named last changes fastest.
Arguments:
- hidden_states: bfloat16 [512, 4096], P('grp', 'kv'), may hold values from -6 to 6
- attn_gain: float32 [4096], P('kv'), may hold values from 0.25 to 1.75
- mlp_gain: float32 [4096], replicated, may hold values from 0.25 to 1.75
- w_query: bfloat16 [4096, 4096], P('kv', 'tp'), may hold values from -0.09375 to 0.09375
- w_out: bfloat16 [32, 128, 4096], P('tp', 'kv'), may hold values from -1 to 1
- w_gate: bfloat16 [4096, 14336], P(None, ('kv', 'tp')), may hold values from -0.09375 to 0.09375
- w_up: bfloat16 [4096, 14336], P(None, ('kv', 'tp')), may hold values from -0.09375 to 0.09375
- w_down: bfloat16 [14336, 4096], P(('kv', 'tp')), may hold values from -0.046875 to 0.046875
- kv_pool: bfloat16 [256, 2, 128, 1024], P(('grp', 'kv'), None, None, 'tp'), may hold values from -110 to 110
- resident_cache: bfloat16 [4, 32, 2, 128, 1024], P('grp', 'kv', None, None, 'tp'), may hold values from -110 to 110
- resident_slot: int32 [4, 32], P('grp', 'kv'), may hold values from 0 to 127
- resident_len: int32 [4, 32], P('grp', 'kv'), may hold values from 1 to 128
- new_owner: int32 [4, 64], replicated, may hold values from 0 to 15, as said below
- new_local: int32 [4, 64], replicated, may hold values from 0 to 15
- new_slot: int32 [4, 64], P('grp', 'kv'), may hold values from 0 to 127
- new_len: int32 [4, 64], P('grp', 'kv'), may hold values from 1 to 128
- token_kv: bfloat16 [512, 2, 1024], P('grp', None, 'tp'), may hold values from -6 to 6
Outputs:
- mixed: bfloat16 [512, 4096], P(('grp', 'kv', 'tp'))
- new_cache: bfloat16 [4, 64, 2, 128, 1024], P('grp', 'kv', None, None, 'tp')
Inputs may be any that keep to these rules, and one draw needn't show every extreme that they name: New page c of group g is kept by the device of kv index c // 16 of group g and comes from the device whose index along grp+kv is new_owner[g, c]; every decode device receives exactly 4 new pages from the owners of each grp index; no owner sends more than 4 pages to the devices of one kv index over all groups, so at most 4 to one device; every owner sends each of its 16 pages exactly once.
All inputs are finite; a program needn't handle non-finite values.
Results may differ from a plain program's by a relative error of at most 0.018.
Values may be sent and summed in bfloat16 or wider, within the bound.
No kernel may reach another device: no remote copies, remote signals or barrier semaphores. Data moves between devices by JAX's collectives and lax.ppermute only.
A program may use at most 128 MiB of HBM per device.

v0:
```python
import jax
import jax.numpy as jnp
from jax import lax
from jax.sharding import PartitionSpec as P

D = 4096
HEADS = 32
KV_HEADS = 8
HEAD_DIM = 128
NPR = 4
neg_fill = -1e30
norm_eps = 1e-05


def combined_all(part, axis, combine):
    gathered = jax.tree.map(lambda a: lax.all_gather(a, axis), part)

    def take(source):
        return jax.tree.map(lambda a: lax.dynamic_index_in_dim(a, source, 0, False), gathered)

    return lax.fori_loop(
        1, lax.axis_size(axis), lambda source, state: combine(state, take(source)), take(0)
    )


def combine(earlier, later):
    top_a, sum_a, acc_a = earlier
    top_b, sum_b, acc_b = later
    top = jnp.maximum(top_a, top_b)
    fade_a = jnp.exp(top_a - top)
    fade_b = jnp.exp(top_b - top)
    return (
        top,
        sum_a * fade_a + sum_b * fade_b,
        acc_a * fade_a[..., None] + acc_b * fade_b[..., None],
    )


def nth_match(table, wanted, places):
    matched = (table == wanted).astype(jnp.int32)
    ranking = jnp.cumsum(matched, axis=1) - 1
    return (matched[:, None, :] == 1) & (ranking[:, None, :] == places[None, :, None])


def move_pages(kv_pool, new_owner, new_local):
    groups = lax.axis_size("grp")
    ranks = lax.axis_size("kv")
    per_dev = new_owner.shape[1] // ranks
    cap = groups * NPR // ranks
    grp_rank = lax.axis_index("grp")
    kv_rank = lax.axis_index("kv")
    owners = new_owner.reshape(groups * ranks, per_dev)
    myself = grp_rank * ranks + kv_rank
    places = jnp.arange(cap, dtype=jnp.int32)
    mine = lax.dynamic_index_in_dim(owners, myself, 0, keepdims=False)
    order = jnp.arange(per_dev, dtype=jnp.int32)
    by_col = (
        new_owner.reshape(groups, ranks, per_dev)
        .transpose(1, 0, 2)
        .reshape(ranks, groups * per_dev)
    )
    local_col = (
        new_local.reshape(groups, ranks, per_dev)
        .transpose(1, 0, 2)
        .reshape(ranks, groups * per_dev)
    )
    select = nth_match(by_col, myself, places)
    picked = jnp.sum(jnp.where(select, local_col[:, None, :], 0), axis=2)
    outgoing = jnp.take(kv_pool, picked.reshape(-1), axis=0)
    received = lax.all_to_all(outgoing, "kv", split_axis=0, concat_axis=0, tiled=True)
    row_here = lax.dynamic_index_in_dim(by_col, kv_rank, 0, keepdims=False)
    sources = grp_rank * ranks + jnp.arange(ranks, dtype=jnp.int32)
    hits = nth_match(
        jnp.broadcast_to(row_here[None, :], (ranks, row_here.shape[0])), sources[:, None], places
    )
    spots = jnp.arange(row_here.shape[0], dtype=jnp.int32)
    where_f = jnp.sum(jnp.where(hits, spots[None, None, :], 0), axis=2).reshape(-1)
    dest_grp = where_f // per_dev
    dest_pos = where_f % per_dev
    same = (dest_grp[:, None] == dest_grp[None, :]) & (dest_pos[:, None] < dest_pos[None, :])
    rank_in = jnp.sum(same.astype(jnp.int32), axis=0)
    target = dest_grp * NPR + rank_in
    items = jnp.arange(target.shape[0], dtype=jnp.int32)
    inverse = jnp.sum(jnp.where(target[None, :] == items[:, None], items[None, :], 0), axis=1)
    sorted_pages = jnp.take(received, inverse, axis=0)
    arrived = lax.all_to_all(sorted_pages, "grp", split_axis=0, concat_axis=0, tiled=True)
    src_grp = mine // ranks
    earlier = (src_grp[:, None] == src_grp[None, :]) & (order[:, None] < order[None, :])
    before = jnp.sum(earlier.astype(jnp.int32), axis=0)
    return jnp.take(arrived, src_grp * NPR + before, axis=0)


def local_partials(query, resident, arrived, res_slot, res_len, arr_slot, arr_len, token_kv, first):
    pages = jnp.concatenate([resident, arrived], axis=0)
    owner_slot = jnp.concatenate([res_slot, arr_slot])
    filled = jnp.concatenate([res_len, arr_len])
    count = pages.shape[0]
    tokens = pages.shape[2]
    kv_here = pages.shape[3] // HEAD_DIM
    slots = query.shape[0]
    ratio = HEADS // KV_HEADS
    keys = pages[:, 0].astype(jnp.float32).reshape(count, tokens, kv_here, HEAD_DIM)
    values = pages[:, 1].astype(jnp.float32).reshape(count, tokens, kv_here, HEAD_DIM)
    grouped = query.reshape(slots, kv_here, ratio, HEAD_DIM)
    picked = jnp.take(grouped, owner_slot, axis=0)
    scores = jnp.einsum("ikgd,itkd->ikgt", picked, keys, precision=lax.Precision.HIGHEST)
    usable = (jnp.arange(tokens, dtype=jnp.int32)[None, :] < filled[:, None])[:, None, None, :]
    scores = jnp.where(usable, scores, neg_fill)
    page_top = jnp.max(scores, axis=3)
    member = owner_slot[None, :] == jnp.arange(slots, dtype=jnp.int32)[:, None]
    slot_top = jnp.max(jnp.where(member[:, :, None, None], page_top[None], neg_fill), axis=1)
    own_keys = token_kv[:, 0].astype(jnp.float32).reshape(slots, kv_here, HEAD_DIM)
    own_values = token_kv[:, 1].astype(jnp.float32).reshape(slots, kv_here, HEAD_DIM)
    own_score = jnp.einsum("skgd,skd->skg", grouped, own_keys, precision=lax.Precision.HIGHEST)
    own_score = jnp.where(first, own_score, neg_fill)
    slot_top = jnp.maximum(slot_top, own_score)
    reach = jnp.take(slot_top, owner_slot, axis=0)
    weights = jnp.where(usable, jnp.exp(scores - reach[..., None]), 0.0)
    page_sum = jnp.sum(weights, axis=3)
    page_acc = jnp.einsum("ikgt,itkd->ikgd", weights, values, precision=lax.Precision.HIGHEST)
    own_weight = jnp.where(first, jnp.exp(own_score - slot_top), 0.0)
    member_f = member.astype(jnp.float32)
    total = jnp.dot(member_f, page_sum.reshape(count, -1), precision=lax.Precision.HIGHEST)
    total = total + own_weight.reshape(slots, -1)
    weighted = jnp.dot(member_f, page_acc.reshape(count, -1), precision=lax.Precision.HIGHEST)
    weighted = (
        weighted.reshape(slots, kv_here, ratio, HEAD_DIM)
        + own_weight[..., None] * own_values[:, :, None, :]
    )
    return (slot_top.reshape(slots, -1), total, weighted.reshape(slots, kv_here * ratio, HEAD_DIM))


def per_device(
    hidden_states,
    attn_gain,
    mlp_gain,
    w_query,
    w_out,
    w_gate,
    w_up,
    w_down,
    kv_pool,
    resident_cache,
    resident_slot,
    resident_len,
    new_owner,
    new_local,
    new_slot,
    new_len,
    token_kv,
):
    ranks = lax.axis_size("kv")
    pairs = lax.axis_size("tp")
    kv_rank = lax.axis_index("kv")
    tp_rank = lax.axis_index("tp")
    features = hidden_states.astype(jnp.float32)
    partial_query = jnp.dot(
        (features * attn_gain).astype(jnp.bfloat16), w_query, preferred_element_type=jnp.float32
    )
    squares = jnp.sum(features * features, axis=1)
    partial_query, squares = lax.psum((partial_query, squares), "kv")
    attn_scale = lax.rsqrt(squares / D + norm_eps)
    query = partial_query * attn_scale[:, None] * HEAD_DIM ** (-0.5)
    new_pages = move_pages(kv_pool, new_owner, new_local)
    top, total, weighted = local_partials(
        query,
        resident_cache[0],
        new_pages,
        resident_slot[0],
        resident_len[0],
        new_slot[0],
        new_len[0],
        token_kv,
        kv_rank == 0,
    )
    top, total, weighted = combined_all((top, total, weighted), "kv", combine)
    attn = (weighted / total[..., None]).astype(jnp.bfloat16)
    slots = attn.shape[0]
    heads_here = attn.shape[1]
    span = HEAD_DIM // ranks
    piece = lax.dynamic_slice_in_dim(attn, kv_rank * span, span, 2)
    branch = jnp.dot(
        piece.reshape(slots, heads_here * span),
        w_out.reshape(heads_here * span, w_out.shape[2]),
        preferred_element_type=jnp.float32,
    )
    width_here = hidden_states.shape[1]
    laid = branch.reshape(slots, ranks, width_here)
    spot = (jnp.arange(ranks, dtype=jnp.int32) == kv_rank) & (tp_rank == 0)
    laid = laid + jnp.where(spot[None, :, None], features[:, None, :], 0.0)
    resid = lax.psum(laid.reshape(slots, ranks * width_here).astype(jnp.bfloat16), ("kv", "tp"))
    resid_f = resid.astype(jnp.float32)
    mlp_scale = lax.rsqrt(jnp.sum(resid_f * resid_f, axis=1) / D + norm_eps)
    normed_mlp = (resid_f * mlp_gain).astype(jnp.bfloat16)
    gate = jnp.dot(normed_mlp, w_gate, preferred_element_type=jnp.float32) * mlp_scale[:, None]
    upward = jnp.dot(normed_mlp, w_up, preferred_element_type=jnp.float32) * mlp_scale[:, None]
    hidden_units = (jax.nn.silu(gate) * upward).astype(jnp.bfloat16)
    row_count = slots // (ranks * pairs)
    down = lax.psum_scatter(
        jnp.dot(hidden_units, w_down, preferred_element_type=jnp.float32).astype(jnp.bfloat16),
        ("kv", "tp"),
        scatter_dimension=0,
        tiled=True,
    ).astype(jnp.float32)
    row_start = (kv_rank * pairs + tp_rank) * row_count
    kept = lax.dynamic_slice_in_dim(resid_f, row_start, row_count, 0)
    mixed = (kept + down).astype(jnp.bfloat16)
    return (mixed, new_pages[None])


def solution(mesh):
    return jax.shard_map(
        per_device,
        mesh=mesh,
        in_specs=(
            P("grp", "kv"),
            P("kv"),
            P(),
            P("kv", "tp"),
            P("tp", "kv", None),
            P(None, ("kv", "tp")),
            P(None, ("kv", "tp")),
            P(("kv", "tp"), None),
            P(("grp", "kv"), None, None, "tp"),
            P("grp", "kv", None, None, "tp"),
            P("grp", "kv"),
            P("grp", "kv"),
            P(),
            P(),
            P("grp", "kv"),
            P("grp", "kv"),
            P("grp", None, "tp"),
        ),
        out_specs=(P(("grp", "kv", "tp"), None), P("grp", "kv", None, None, "tp")),
        check_vma=False,
    )
```

profile of v0, /device:TPU:0, one launch (start us, length us, event | category | flops | bytes accessed | tf_op | source)
XLA Modules:
  0.0 407.0 jit_solution(611504076523170792)
XLA Ops:
  7.2 0.8 reshape.445
  7.9 0.8 reshape.450
  8.8 0.2 reduce_window_sum.17
  9.0 0.8 reshape.447
  9.9 0.1 select_reduce_fusion.3
  10.2 5.0 %gather_fusion.2 = bf16[16,2,128,512]{3,2,1,0:T(8,128)(2,1)} fusion(bf16[16,2,128,512]{3,2,1,0:T(8,128)(2,1)} %param.29, s32[1024]{0:T(1024)S(1)} %pad_clamp_fusion.2), kind=kCustom, calls=%fused_computation.clone | custom fusion | bytes 8388672 | tf_op jit(solution)/shard_map/jit(_take)/gather | solution.py:69
  15.2 4.7 %broadcast_select_fusion.2 = bf16[16,2,128,512]{3,2,1,0:T(8,128)(2,1)} fusion(bf16[16,2,128,512]{3,2,1,0:T(8,128)(2,1)} %gather_fusion.2, pred[16]{0:T(512)(128)(4,1)S(1)} %compare_and_fusion.2), kind=kLoop, calls=%fused_computation.18 | loop fusion | flops 2097152 | bytes 8388624 | tf_op jit(solution)/shard_map/jit(_take)/select_n | solution.py:69
  19.9 5.2 %all-to-all-start = ((bf16[16,2,128,512]{3,2,1,0:T(8,128)(2,1)}), bf16[16,2,128,512]{3,2,1,0:T(8,128)(2,1)}, u32[]{:S(2)}, u32[]{:S(2)}) async-start(bf16[16,2,128,512]{3,2,1,0:T(8,128)(2,1)} %broadcast_select_fusion.2), calls=%async_computation | async-start | bytes 8388608 | tf_op jit(solution)/shard_map/all_to_all | solution.py:70
  25.1 0.2 reduce_window_sum.18
  25.4 0.1 select_reduce_fusion.2
  25.9 47.8 %all-to-all-done = bf16[16,2,128,512]{3,2,1,0:T(8,128)(2,1)} async-done(((bf16[16,2,128,512]{3,2,1,0:T(8,128)(2,1)}), bf16[16,2,128,512]{3,2,1,0:T(8,128)(2,1)}, u32[]{:S(2)}, u32[]{:S(2)}) %all-to-all-start) | async-done | bytes 4194336 | tf_op jit(solution)/shard_map/all_to_all | solution.py:70
  73.7 5.0 %gather_fusion.3 = bf16[16,2,128,512]{3,2,1,0:T(8,128)(2,1)} fusion(bf16[16,2,128,512]{3,2,1,0:T(8,128)(2,1)} %all-to-all-done, s32[1024]{0:T(1024)S(1)} %pad_clamp_fusion.1), kind=kCustom, calls=%fused_computation.1.clone | custom fusion | bytes 8388672 | tf_op jit(solution)/shard_map/jit(_take)/gather | solution.py:85
  78.7 4.7 %broadcast_select_fusion.1 = bf16[16,2,128,512]{3,2,1,0:T(8,128)(2,1)} fusion(bf16[16,2,128,512]{3,2,1,0:T(8,128)(2,1)} %gather_fusion.3, pred[16]{0:T(512)(128)(4,1)S(1)} %compare_and_fusion.1), kind=kLoop, calls=%fused_computation.17 | loop fusion | flops 2097152 | bytes 8388624 | tf_op jit(solution)/shard_map/jit(_take)/select_n | solution.py:85
  83.4 5.2 %all-to-all-start.1 = ((bf16[16,2,128,512]{3,2,1,0:T(8,128)(2,1)}), bf16[16,2,128,512]{3,2,1,0:T(8,128)(2,1)}, u32[]{:S(2)}, u32[]{:S(2)}) async-start(bf16[16,2,128,512]{3,2,1,0:T(8,128)(2,1)} %broadcast_select_fusion.1), calls=%async_computation.1 | async-start | bytes 8388608 | tf_op jit(solution)/shard_map/all_to_all | solution.py:86
  88.7 4.0 fusion.7
  93.1 0.4 slice_convert_fusion
  93.5 0.2 copy.150
  93.7 0.2 copy.143
  93.9 0.7 copy.134
  94.6 9.3 %psum.22 = f32[128]{0:T(128)S(1)} all-reduce(f32[128]{0:T(128)S(1)} %multiply_reduce_fusion.1), channel_id=1, replica_groups=mesh['grp'=4,'kv'=4,'tp'=2] {'kv'}, use_global_device_ids=true, to_apply=%region_2.0 | all-reduce | flops 128 | bytes 1024 | tf_op jit(solution)/shard_map/psum | solution.py:161
  104.2 41.8 %all-reduce.3.cloned.1.call-done = f32[128,2048]{1,0:T(8,128)} async-done(((f32[128,2048]{1,0:T(8,128)}), f32[128,2048]{1,0:T(8,128)}) %all-reduce.3.cloned.1.call-update) | async-done | bytes 1048592 | tf_op jit(solution)/shard_map/psum | solution.py:161
  145.9 1.4 multiply_multiply_fusion
  147.3 0.7 reshape.444
  148.0 1.3 gather_fusion
  149.4 2.5 fusion.34
  151.9 29.4 %all-to-all-done.1 = bf16[16,2,128,512]{3,2,1,0:T(8,128)(2,1)} async-done(((bf16[16,2,128,512]{3,2,1,0:T(8,128)(2,1)}), bf16[16,2,128,512]{3,2,1,0:T(8,128)(2,1)}, u32[]{:S(2)}, u32[]{:S(2)}) %all-to-all-start.1) | async-done | bytes 4194336 | tf_op jit(solution)/shard_map/all_to_all | solution.py:86
  181.3 5.0 %gather_fusion.4 = bf16[16,2,128,512]{3,2,1,0:T(8,128)(2,1)} fusion(bf16[16,2,128,512]{3,2,1,0:T(8,128)(2,1)} %all-to-all-done.1, s32[1024]{0:T(1024)S(1)} %pad_clamp_fusion), kind=kCustom, calls=%fused_computation.2.clone | custom fusion | bytes 8388672 | tf_op jit(solution)/shard_map/jit(_take)/gather | solution.py:90
  186.3 2.8 broadcast_select_fusion
  189.1 2.9 pad_maximum_fusion
  192.0 3.5 copy.122
  195.5 4.2 %fusion.33 = (f32[24,4,4]{2,1,0:T(4,128)S(1)}, f32[24,4,4,128]{3,2,1,0:T(4,128)}) fusion(bf16[24,128,4,128]{1,3,2,0:T(8,128)(2,1)S(1)} %bitcast.91, f32[24,4,4,128]{3,2,1,0:T(4,128)} %gather_fusion, pred[24]{0:T(512)(128)(4,1)S(1)} %get-tuple-element.244, pred[24,128]{1,0:T(8,128)(4,1)S(1)} %iota_compare_fusion), kind=kOutput, calls=%fused_computation.125 | convolution fusion | flops 75644544 | bytes 3543576 | tf_op jit(solution)/shard_map/ikgd,itkd->ikgt/dot_general | solution.py:106
  200.0 0.2 copy.126
  200.2 1.8 exponential_select_fusion
  202.0 0.6 gather_fusion.1
  202.7 3.5 copy.130
  206.2 6.6 %fusion.13 = f32[24,4,4,128]{3,2,1,0:T(4,128)} fusion(bf16[24,128,4,128]{1,3,2,0:T(8,128)(2,1)S(1)} %bitcast.95, f32[24,4,4,128]{3,2,1,0:T(4,128)} %get-tuple-element.261, f32[24,4,4]{2,1,0:T(4,128)S(1)} %broadcast_select_fusion.3, pred[24,128]{1,0:T(8,128)(4,1)S(1)} %iota_compare_fusion), kind=kOutput, calls=%fused_computation.50 | convolution fusion | flops 75595776 | bytes 3543552 | tf_op jit(solution)/shard_map/ikgt,itkd->ikgd/dot_general | solution.py:120
  212.8 1.0 reshape.456
  214.0 1.0 copy.129
  215.0 1.7 convolution_add_fusion
  216.8 1.7 copy.135
  218.5 0.3 all-reduce.5.cloned.1.call-start
  218.8 6.7 %copy.138 = bf16[4096,512]{1,0:T(8,128)(2,1)} copy(bf16[4096,512]{0,1:T(8,128)(2,1)} %bitcast.92) | data formatting | bytes 8388608 | tf_op jit(solution)/shard_map/dot_general | solution.py:182
  225.5 0.4 fusion.14
  226.0 0.2 convolution_add_fusion.1
  226.2 8.0 %all-gather = f32[512,16]{0,1:T(8,128)S(1)} all-gather(f32[128,16]{0,1:T(8,128)S(1)} %convolution_add_fusion.1), channel_id=2, replica_groups=mesh['grp'=4,'kv'=4,'tp'=2] {'kv'}, dimensions={0}, use_global_device_ids=true | all-gather | bytes 40960 | tf_op jit(solution)/shard_map/all_gather | solution.py:16
  234.3 8.2 %all_gather.12 = f32[4,128,16]{1,2,0:T(8,128)S(1)} all-gather(f32[1,128,16]{1,2,0:T(8,128)S(1)} %bitcast.104), channel_id=1, replica_groups=mesh['grp'=4,'kv'=4,'tp'=2] {'kv'}, dimensions={0}, use_global_device_ids=true | all-gather | bytes 40960 | tf_op jit(solution)/shard_map/all_gather | solution.py:16
  242.5 26.1 %all-gather.3.cloned.1.call-done = f32[4,128,16,128]{3,2,1,0:T(8,128)} async-done(((f32[1,128,16,128]{3,2,1,0:T(8,128)}), f32[4,128,16,128]{3,2,1,0:T(8,128)}) %all-gather.3.cloned.1.call-update) | async-done | bytes 4194320 | tf_op jit(solution)/shard_map/all_gather | solution.py:16
  268.7 1.3 slice_bitcast_fusion
  270.0 6.5 %while.19 = (s32[]{:T(128)}, f32[128,16]{0,1:T(8,128)S(1)}, f32[128,16]{0,1:T(8,128)S(1)}, f32[128,16,128]{2,1,0:T(8,128)S(1)}, f32[4,128,16]{1,2,0:T(8,128)S(1)...) while((s32[]{:T(128)}, f32[128,16]{0,1:T(8,128)S(1)}, ...), condition=%wide.region_14.16_spmd, body=%wide.region_13.15_spmd.sunk | while | flops 798725 | bytes 3276955 | solution.py:21
  270.2 1.9 fusion.48
  272.4 1.9 fusion.48
  274.5 1.9 fusion.48
  276.5 0.4 copy.137
  276.9 3.7 add_convert_fusion
  280.7 0.7 copy.140
  281.3 1.4 copy.141
  282.7 56.8 %all-reduce.5.cloned.1.call-done = bf16[128,4096]{1,0:T(8,128)(2,1)} async-done(((bf16[128,4096]{1,0:T(8,128)(2,1)}), bf16[128,4096]{1,0:T(8,128)(2,1)}) %all-reduce.5.cloned.1.call-update) | async-done | bytes 1048592 | tf_op jit(solution)/shard_map/psum | solution.py:191
  339.6 1.5 multiply_reduce_fusion
  341.1 7.7 %convolution_multiply_fusion.1 = f32[128,1792]{1,0:T(8,128)S(1)} fusion(bf16[4096,1792]{1,0:T(8,128)(2,1)} %param.26, f32[4096]{0:T(1024)S(1)} %copy-done.7, bf16[128,4096]{1,0:T(8,128)(2,1)} %all-reduce.5.cloned.1.call-done, f32[128]{0:T(128)S(1)} %add_rsqrt_fusion), kind=kOutput, calls=%fused_computation.22 | convolution fusion | flops 1880850432 | bytes 16663040 | tf_op jit(solution)/shard_map/dot_general | solution.py:195
  348.8 14.8 %convolution_convert_fusion = bf16[128,4096]{1,0:T(8,128)(2,1)} fusion(bf16[1792,4096]{1,0:T(8,128)(2,1)} %param.28, bf16[4096,1792]{1,0:T(8,128)(2,1)} %param.27, f32[128,1792]{1,0:T(8,128)S(1)} %convolution_multiply_fusion.1, f32[4096]{0:T(1024)S(1)} %copy-done.7, bf16[128,4096]{1,0:T(8,128)(2,1)S(1)} %copy-done, f32[128]{0:T(128)S(1)} %add_rsqrt_fusion), kind=kOutput, calls=%fused_computation.15 | convolution fusion | flops 3761799168 | bytes 32391680 | tf_op jit(solution)/shard_map/dot_general | solution.py:200
  363.6 4.7 %fusion.46 = bf16[1,16,2,128,512]{4,3,2,1,0:T(8,128)(2,1)} fusion(bf16[16,2,128,512]{3,2,1,0:T(8,128)(2,1)} %gather_fusion.4, pred[16]{0:T(512)(128)(4,1)S(1)} %get-tuple-element.246), kind=kLoop, calls=%fused_computation.127 | loop fusion | flops 2097152 | bytes 8388624 | tf_op jit(solution)/shard_map/broadcast_in_dim | solution.py:208
  368.2 0.2 convert_element_type.86
  368.4 30.5 %reduce-scatter.2.cloned.1.call-done = bf16[16,4096]{1,0:T(8,128)(2,1)} async-done(((bf16[128,4096]{1,0:T(8,128)(2,1)}), bf16[16,4096]{1,0:T(8,128)(2,1)}) %reduce-scatter.2.cloned.1.call-update) | async-done | bytes 131088 | tf_op jit(solution)/shard_map/reduce_scatter | solution.py:199
  398.9 1.6 add_convert_fusion.1
  (92 shorter events, 3.2 us)
Async XLA Ops:
  19.9 53.8 %all-to-all-start = ((bf16[16,2,128,512]{3,2,1,0:T(8,128)(2,1)}), bf16[16,2,128,512]{3,2,1,0:T(8,128)(2,1)}, u32[]{:S(2)}, u32[]{:S(2)}) async-start(bf16[16,2,128,512]{3,2,1,0:T(8,128)(2,1)} %broadcast_select_fusion.2), calls=%async_computation | async-start | bytes 8388608 | tf_op jit(solution)/shard_map/all_to_all | solution.py:70
  83.4 5.3 %copy-start.1 = (bf16[128,1024]{1,0:T(8,128)(2,1)S(1)}, bf16[128,1024]{1,0:T(8,128)(2,1)}, u32[]{:S(2)}) copy-start(bf16[128,1024]{1,0:T(8,128)(2,1)} %param.21) | copy-start | bytes 786436
  83.4 5.3 %copy-start.8 = (f32[1024]{0:T(1024)S(1)}, f32[1024]{0:T(1024)}, u32[]{:S(2)}) copy-start(f32[1024]{0:T(1024)} %param.22) | copy-start | bytes 12292
  83.4 97.9 %all-to-all-start.1 = ((bf16[16,2,128,512]{3,2,1,0:T(8,128)(2,1)}), bf16[16,2,128,512]{3,2,1,0:T(8,128)(2,1)}, u32[]{:S(2)}, u32[]{:S(2)}) async-start(bf16[16,2,128,512]{3,2,1,0:T(8,128)(2,1)} %broadcast_select_fusion.1), calls=%async_computation.1 | async-start | bytes 8388608 | tf_op jit(solution)/shard_map/all_to_all | solution.py:86
  88.6 4.2 %copy-start.9 = (s32[1,16]{1,0:T(1,128)S(1)}, s32[1,16]{1,0:T(1,128)}, u32[]{:S(2)}) copy-start(s32[1,16]{1,0:T(1,128)} %param.35) | copy-start | bytes 196
  88.6 4.2 %copy-start.10 = (s32[1,8]{1,0:T(1,128)S(1)}, s32[1,8]{1,0:T(1,128)}, u32[]{:S(2)}) copy-start(s32[1,8]{1,0:T(1,128)} %param.31) | copy-start | bytes 100
  88.6 4.5 %copy-start.5 = (bf16[128,2,512]{2,1,0:T(2,128)(2,1)S(1)}, bf16[128,2,512]{2,1,0:T(2,128)(2,1)}, u32[]{:S(2)}) copy-start(bf16[128,2,512]{2,1,0:T(2,128)(2,1)} %param.37) | copy-start | bytes 786436
  88.6 4.9 %copy-start.11 = (s32[1,16]{1,0:T(1,128)S(1)}, s32[1,16]{1,0:T(1,128)}, u32[]{:S(2)}) copy-start(s32[1,16]{1,0:T(1,128)} %param.36) | copy-start | bytes 196
  88.6 4.9 %copy-start.12 = (s32[1,8]{1,0:T(1,128)S(1)}, s32[1,8]{1,0:T(1,128)}, u32[]{:S(2)}) copy-start(s32[1,8]{1,0:T(1,128)} %param.32) | copy-start | bytes 100
  88.6 57.3 %all-reduce.3.cloned.1.call-start = ((), (), s32[]{:S(2)}) async-start(), calls=%async_computation.3 | async-start | bytes 2097152 | tf_op jit(solution)/shard_map/psum | solution.py:161
  92.7 176.0 %all-gather.3.cloned.1.call-start = ((), (), s32[]{:S(2)}) async-start(), calls=%async_computation.4 | async-start | bytes 5242880 | tf_op jit(solution)/shard_map/all_gather | solution.py:16
  186.3 2.9 copy-start.2
  202.0 0.7 copy-start.3
  218.5 121.1 %all-reduce.5.cloned.1.call-start = ((), (), s32[]{:S(2)}) async-start(), calls=%async_computation.5 | async-start | bytes 2097152 | tf_op jit(solution)/shard_map/psum | solution.py:191
  218.8 6.7 %copy-start.6 = (f32[24,4,4,128]{3,2,1,0:T(4,128)S(1)}, f32[24,4,4,128]{3,2,1,0:T(4,128)}, u32[]{:S(2)}) copy-start(f32[24,4,4,128]{3,2,1,0:T(4,128)} %get-tuple-element.261) | copy-start | bytes 589828
  218.8 15.4 %copy-start.4 = (f32[128,4,4]{2,1,0:T(4,128)S(1)}, f32[128,4,4]{2,1,0:T(4,128)}, u32[]{:S(2)}) copy-start(f32[128,4,4]{2,1,0:T(4,128)} %copy-done.3) | copy-start | bytes 24580
  280.6 60.4 %copy-start.7 = (f32[4096]{0:T(1024)S(1)}, f32[4096]{0:T(1024)}, u32[]{:S(2)}) copy-start(f32[4096]{0:T(1024)} %param.23) | copy-start | bytes 49156
  282.7 116.2 %reduce-scatter.2.cloned.1.call-start = ((), (), s32[]{:S(2)}) async-start(), calls=%async_computation.6 | async-start | bytes 1179648 | tf_op jit(solution)/shard_map/reduce_scatter | solution.py:199
  341.1 7.7 %copy-start = (bf16[128,4096]{1,0:T(8,128)(2,1)S(1)}, bf16[128,4096]{1,0:T(8,128)(2,1)}, u32[]{:S(2)}) copy-start(bf16[128,4096]{1,0:T(8,128)(2,1)} %all-reduce.5.cloned.1.call-done) | copy-start | bytes 3145732
Sparse Core Ops, SparseCore 0:
  92.8 53.0 all-reduce.2
  218.6 50.0 all-gather.2
  282.8 56.6 all-reduce.4
  363.7 35.1 reduce-scatter.1
where the time goes:
time: 408 us; the launch traced here: 407 us
  waiting for transfers between devices  232 us (57%)
  matrix products  45.4 us (11%)
  local copies, waits for them, and re-layouts  43.9 us (11%)
  other arithmetic  34.8 us (9%)
  blocking collectives  25.5 us (6%)
  between operations  14.2 us (3%)
  starting transfers between devices  10.8 us (3%)
    psum x1, waiting for transfers between devices, per_device(): lax.psum(laid.reshape(slots, ranks * width_here).astype(jnp.bfloat16), ('...  56.8 us
    all_to_all x1, waiting for transfers between devices, move_pages(): lax.all_to_all(outgoing, 'kv', split_axis=0, concat_axis=0, tiled=True)  47.8 us
    psum x1, waiting for transfers between devices, per_device(): partial_query, squares = lax.psum((partial_query, squares), 'kv')  41.8 us
    reduce_scatter x1, waiting for transfers between devices, per_device(): lax.psum_scatter(jnp.dot(hidden_units, w_down, preferred_element_type=jnp...  30.5 us
    all_to_all x1, waiting for transfers between devices, move_pages(): lax.all_to_all(sorted_pages, 'grp', split_axis=0, concat_axis=0, tiled=True)  29.4 us
    all_gather x1, waiting for transfers between devices, combined_all(): gathered = jax.tree.map(lambda a: lax.all_gather(a, axis), part)  26.1 us
    all_gather x2, blocking collectives, combined_all(): gathered = jax.tree.map(lambda a: lax.all_gather(a, axis), part)  16.2 us
    dot_general x1, matrix products, per_device(): jnp.dot(hidden_units, w_down, preferred_element_type=jnp.float32)  14.8 us
  transfers between devices with their start and end apart: 6, of which 6 were waited for; matrix products, arithmetic and copies ran while one was open for 6% of the time, Pallas kernels for 0%

commit v1 on v0

--- a/solution.py
+++ b/solution.py
@@ -188,7 +188,10 @@
     laid = branch.reshape(slots, ranks, width_here)
     spot = (jnp.arange(ranks, dtype=jnp.int32) == kv_rank) & (tp_rank == 0)
     laid = laid + jnp.where(spot[None, :, None], features[:, None, :], 0.0)
-    resid = lax.psum(laid.reshape(slots, ranks * width_here).astype(jnp.bfloat16), ("kv", "tp"))
+    convert_paths = lambda inp, axis_id, ax_name: lax.psum(lax.psum(inp, axis_id), ax_name)
+    resid = convert_paths(
+        laid.reshape(slots, ranks * width_here).astype(jnp.bfloat16), "kv", ax_name="tp"
+    )
     resid_f = resid.astype(jnp.float32)
     mlp_scale = lax.rsqrt(jnp.sum(resid_f * resid_f, axis=1) / D + norm_eps)
     normed_mlp = (resid_f * mlp_gain).astype(jnp.bfloat16)

time: 408 us -> 428 us (1.049)
  waiting for transfers between devices: 232 us -> 252 us
    psum x1 -> x2, waiting for transfers between devices: 56.8 us -> 74.2 us  [the longest x1 52.6 us: per_device(): lax.psum(inp, axis_id)]
  transfers between devices with their start and end apart: 6 -> 7, of which waited for: 6 -> 7; matrix products, arithmetic and copies ran while one was open for 6% -> 6% of each run, Pallas kernels for 0% -> 0%
where the time goes in v1:
time: 428 us; the launch traced here: 426 us
  waiting for transfers between devices  252 us (59%)
  matrix products  45.4 us (11%)
  local copies, waits for them, and re-layouts  43.9 us (10%)
  other arithmetic  34.8 us (8%)
  blocking collectives  25.5 us (6%)
  between operations  14.2 us (3%)
  starting transfers between devices  10.8 us (3%)
    psum x1, waiting for transfers between devices, per_device(): lax.psum(inp, axis_id)  52.6 us
    all_to_all x1, waiting for transfers between devices, move_pages(): lax.all_to_all(outgoing, 'kv', split_axis=0, concat_axis=0, tiled=True)  47.8 us
    psum x1, waiting for transfers between devices, per_device(): partial_query, squares = lax.psum((partial_query, squares), 'kv')  41.8 us
    reduce_scatter x1, waiting for transfers between devices, per_device(): lax.psum_scatter(jnp.dot(hidden_units, w_down, preferred_element_type=jnp...  32.5 us
    all_to_all x1, waiting for transfers between devices, move_pages(): lax.all_to_all(sorted_pages, 'grp', split_axis=0, concat_axis=0, tiled=True)  29.4 us
    all_gather x1, waiting for transfers between devices, combined_all(): gathered = jax.tree.map(lambda a: lax.all_gather(a, axis), part)  26.1 us
    psum x1, waiting for transfers between devices, per_device(): lax.psum(lax.psum(inp, axis_id), ax_name)  21.6 us
    all_gather x2, blocking collectives, combined_all(): gathered = jax.tree.map(lambda a: lax.all_gather(a, axis), part)  16.2 us
  transfers between devices with their start and end apart: 7, of which 7 were waited for; matrix products, arithmetic and copies ran while one was open for 6% of the time, Pallas kernels for 0%

profile of v1, /device:TPU:0, one launch (start us, length us, event | category | flops | bytes accessed | tf_op | source)
XLA Modules:
  0.0 426.4 jit_solution(12903447836001095920)
XLA Ops:
  7.2 0.8 reshape.445
  7.9 0.8 reshape.450
  8.8 0.2 reduce_window_sum.17
  9.0 0.8 reshape.447
  9.9 0.1 select_reduce_fusion.3
  10.2 5.0 %gather_fusion.2 = bf16[16,2,128,512]{3,2,1,0:T(8,128)(2,1)} fusion(bf16[16,2,128,512]{3,2,1,0:T(8,128)(2,1)} %param.29, s32[1024]{0:T(1024)S(1)} %pad_clamp_fusion.2), kind=kCustom, calls=%fused_computation.clone | custom fusion | bytes 8388672 | tf_op jit(solution)/shard_map/jit(_take)/gather | solution.py:69
  15.2 4.7 %broadcast_select_fusion.2 = bf16[16,2,128,512]{3,2,1,0:T(8,128)(2,1)} fusion(bf16[16,2,128,512]{3,2,1,0:T(8,128)(2,1)} %gather_fusion.2, pred[16]{0:T(512)(128)(4,1)S(1)} %compare_and_fusion.2), kind=kLoop, calls=%fused_computation.18 | loop fusion | flops 2097152 | bytes 8388624 | tf_op jit(solution)/shard_map/jit(_take)/select_n | solution.py:69
  19.9 5.2 %all-to-all-start = ((bf16[16,2,128,512]{3,2,1,0:T(8,128)(2,1)}), bf16[16,2,128,512]{3,2,1,0:T(8,128)(2,1)}, u32[]{:S(2)}, u32[]{:S(2)}) async-start(bf16[16,2,128,512]{3,2,1,0:T(8,128)(2,1)} %broadcast_select_fusion.2), calls=%async_computation | async-start | bytes 8388608 | tf_op jit(solution)/shard_map/all_to_all | solution.py:70
  25.1 0.2 reduce_window_sum.18
  25.9 47.8 %all-to-all-done = bf16[16,2,128,512]{3,2,1,0:T(8,128)(2,1)} async-done(((bf16[16,2,128,512]{3,2,1,0:T(8,128)(2,1)}), bf16[16,2,128,512]{3,2,1,0:T(8,128)(2,1)}, u32[]{:S(2)}, u32[]{:S(2)}) %all-to-all-start) | async-done | bytes 4194336 | tf_op jit(solution)/shard_map/all_to_all | solution.py:70
  73.7 5.0 %gather_fusion.3 = bf16[16,2,128,512]{3,2,1,0:T(8,128)(2,1)} fusion(bf16[16,2,128,512]{3,2,1,0:T(8,128)(2,1)} %all-to-all-done, s32[1024]{0:T(1024)S(1)} %pad_clamp_fusion.1), kind=kCustom, calls=%fused_computation.1.clone | custom fusion | bytes 8388672 | tf_op jit(solution)/shard_map/jit(_take)/gather | solution.py:85
  78.7 4.7 %broadcast_select_fusion.1 = bf16[16,2,128,512]{3,2,1,0:T(8,128)(2,1)} fusion(bf16[16,2,128,512]{3,2,1,0:T(8,128)(2,1)} %gather_fusion.3, pred[16]{0:T(512)(128)(4,1)S(1)} %compare_and_fusion.1), kind=kLoop, calls=%fused_computation.17 | loop fusion | flops 2097152 | bytes 8388624 | tf_op jit(solution)/shard_map/jit(_take)/select_n | solution.py:85
  83.4 5.2 %all-to-all-start.1 = ((bf16[16,2,128,512]{3,2,1,0:T(8,128)(2,1)}), bf16[16,2,128,512]{3,2,1,0:T(8,128)(2,1)}, u32[]{:S(2)}, u32[]{:S(2)}) async-start(bf16[16,2,128,512]{3,2,1,0:T(8,128)(2,1)} %broadcast_select_fusion.1), calls=%async_computation.1 | async-start | bytes 8388608 | tf_op jit(solution)/shard_map/all_to_all | solution.py:86
  88.7 4.0 fusion.7
  93.1 0.4 slice_convert_fusion
  93.5 0.2 copy.150
  93.7 0.2 copy.143
  93.9 0.7 copy.134
  94.6 9.3 %psum.29 = f32[128]{0:T(128)S(1)} all-reduce(f32[128]{0:T(128)S(1)} %multiply_reduce_fusion.1), channel_id=1, replica_groups=mesh['grp'=4,'kv'=4,'tp'=2] {'kv'}, use_global_device_ids=true, to_apply=%region_2.0 | all-reduce | flops 128 | bytes 1024 | tf_op jit(solution)/shard_map/psum | solution.py:161
  104.2 41.8 %all-reduce.4.cloned.1.call-done = f32[128,2048]{1,0:T(8,128)} async-done(((f32[128,2048]{1,0:T(8,128)}), f32[128,2048]{1,0:T(8,128)}) %all-reduce.4.cloned.1.call-update) | async-done | bytes 1048592 | tf_op jit(solution)/shard_map/psum | solution.py:161
  145.9 1.4 multiply_multiply_fusion
  147.3 0.7 reshape.444
  148.0 1.3 gather_fusion
  149.4 2.5 fusion.34
  151.9 29.4 %all-to-all-done.1 = bf16[16,2,128,512]{3,2,1,0:T(8,128)(2,1)} async-done(((bf16[16,2,128,512]{3,2,1,0:T(8,128)(2,1)}), bf16[16,2,128,512]{3,2,1,0:T(8,128)(2,1)}, u32[]{:S(2)}, u32[]{:S(2)}) %all-to-all-start.1) | async-done | bytes 4194336 | tf_op jit(solution)/shard_map/all_to_all | solution.py:86
  181.3 5.0 %gather_fusion.4 = bf16[16,2,128,512]{3,2,1,0:T(8,128)(2,1)} fusion(bf16[16,2,128,512]{3,2,1,0:T(8,128)(2,1)} %all-to-all-done.1, s32[1024]{0:T(1024)S(1)} %pad_clamp_fusion), kind=kCustom, calls=%fused_computation.2.clone | custom fusion | bytes 8388672 | tf_op jit(solution)/shard_map/jit(_take)/gather | solution.py:90
  186.3 2.8 broadcast_select_fusion
  189.1 2.9 pad_maximum_fusion
  192.0 3.5 copy.122
  195.5 4.2 fusion.33
  200.0 0.2 copy.126
  200.2 1.8 exponential_select_fusion
  202.0 0.6 gather_fusion.1
  202.7 3.5 copy.130
  206.2 6.6 %fusion.13 = f32[24,4,4,128]{3,2,1,0:T(4,128)} fusion(bf16[24,128,4,128]{1,3,2,0:T(8,128)(2,1)S(1)} %bitcast.95, f32[24,4,4,128]{3,2,1,0:T(4,128)} %get-tuple-element.261, f32[24,4,4]{2,1,0:T(4,128)S(1)} %broadcast_select_fusion.3, pred[24,128]{1,0:T(8,128)(4,1)S(1)} %iota_compare_fusion), kind=kOutput, calls=%fused_computation.50 | convolution fusion | flops 75595776 | bytes 3543552 | tf_op jit(solution)/shard_map/ikgt,itkd->ikgd/dot_general | solution.py:120
  212.8 1.0 reshape.456
  214.0 1.0 copy.129
  215.0 1.7 convolution_add_fusion
  216.8 1.7 copy.135
  218.5 0.3 all-reduce.6.cloned.1.call-start
  218.8 6.7 %copy.138 = bf16[4096,512]{1,0:T(8,128)(2,1)} copy(bf16[4096,512]{0,1:T(8,128)(2,1)} %bitcast.92) | data formatting | bytes 8388608 | tf_op jit(solution)/shard_map/dot_general | solution.py:182
  225.5 0.4 fusion.14
  226.0 0.2 convolution_add_fusion.1
  226.2 8.0 %all-gather = f32[512,16]{0,1:T(8,128)S(1)} all-gather(f32[128,16]{0,1:T(8,128)S(1)} %convolution_add_fusion.1), channel_id=2, replica_groups=mesh['grp'=4,'kv'=4,'tp'=2] {'kv'}, dimensions={0}, use_global_device_ids=true | all-gather | bytes 40960 | tf_op jit(solution)/shard_map/all_gather | solution.py:16
  234.3 8.2 %all_gather.12 = f32[4,128,16]{1,2,0:T(8,128)S(1)} all-gather(f32[1,128,16]{1,2,0:T(8,128)S(1)} %bitcast.104), channel_id=1, replica_groups=mesh['grp'=4,'kv'=4,'tp'=2] {'kv'}, dimensions={0}, use_global_device_ids=true | all-gather | bytes 40960 | tf_op jit(solution)/shard_map/all_gather | solution.py:16
  242.5 26.1 %all-gather.3.cloned.1.call-done = f32[4,128,16,128]{3,2,1,0:T(8,128)} async-done(((f32[1,128,16,128]{3,2,1,0:T(8,128)}), f32[4,128,16,128]{3,2,1,0:T(8,128)}) %all-gather.3.cloned.1.call-update) | async-done | bytes 4194320 | tf_op jit(solution)/shard_map/all_gather | solution.py:16
  268.7 1.3 slice_bitcast_fusion
  270.0 6.5 %while.19 = (s32[]{:T(128)}, f32[128,16]{0,1:T(8,128)S(1)}, f32[128,16]{0,1:T(8,128)S(1)}, f32[128,16,128]{2,1,0:T(8,128)S(1)}, f32[4,128,16]{1,2,0:T(8,128)S(1)...) while((s32[]{:T(128)}, f32[128,16]{0,1:T(8,128)S(1)}, ...), condition=%wide.region_14.16_spmd, body=%wide.region_13.15_spmd.sunk | while | flops 798725 | bytes 3276955 | solution.py:21
  270.2 1.9 fusion.48
  272.4 1.9 fusion.48
  274.5 1.9 fusion.48
  276.5 0.4 copy.137
  276.9 3.7 add_convert_fusion
  280.7 0.7 copy.140
  281.3 1.4 copy.141
  282.7 52.6 %all-reduce.6.cloned.1.call-done = bf16[128,4096]{1,0:T(8,128)(2,1)} async-done(((bf16[128,4096]{1,0:T(8,128)(2,1)}), bf16[128,4096]{1,0:T(8,128)(2,1)}) %all-reduce.6.cloned.1.call-update) | async-done | bytes 1048592 | tf_op jit(solution)/shard_map/psum | solution.py:191
  335.4 21.6 %all-reduce.8.cloned.1.call-done = bf16[128,4096]{1,0:T(8,128)(2,1)} async-done(((bf16[128,4096]{1,0:T(8,128)(2,1)}), bf16[128,4096]{1,0:T(8,128)(2,1)}) %all-reduce.8.cloned.1.call-update) | async-done | bytes 1048592 | tf_op jit(solution)/shard_map/psum | solution.py:191
  357.0 1.5 multiply_reduce_fusion
  358.5 7.7 %convolution_multiply_fusion.1 = f32[128,1792]{1,0:T(8,128)S(1)} fusion(bf16[4096,1792]{1,0:T(8,128)(2,1)} %param.26, f32[4096]{0:T(1024)S(1)} %copy-done.7, bf16[128,4096]{1,0:T(8,128)(2,1)} %all-reduce.8.cloned.1.call-done, f32[128]{0:T(128)S(1)} %add_rsqrt_fusion), kind=kOutput, calls=%fused_computation.22 | convolution fusion | flops 1880850432 | bytes 16663040 | tf_op jit(solution)/shard_map/dot_general | solution.py:198
  366.2 14.8 %convolution_convert_fusion = bf16[128,4096]{1,0:T(8,128)(2,1)} fusion(bf16[1792,4096]{1,0:T(8,128)(2,1)} %param.28, bf16[4096,1792]{1,0:T(8,128)(2,1)} %param.27, f32[128,1792]{1,0:T(8,128)S(1)} %convolution_multiply_fusion.1, f32[4096]{0:T(1024)S(1)} %copy-done.7, bf16[128,4096]{1,0:T(8,128)(2,1)S(1)} %copy-done, f32[128]{0:T(128)S(1)} %add_rsqrt_fusion), kind=kOutput, calls=%fused_computation.15 | convolution fusion | flops 3761799168 | bytes 32391680 | tf_op jit(solution)/shard_map/dot_general | solution.py:203
  381.0 4.7 %fusion.46 = bf16[1,16,2,128,512]{4,3,2,1,0:T(8,128)(2,1)} fusion(bf16[16,2,128,512]{3,2,1,0:T(8,128)(2,1)} %gather_fusion.4, pred[16]{0:T(512)(128)(4,1)S(1)} %get-tuple-element.246), kind=kLoop, calls=%fused_computation.127 | loop fusion | flops 2097152 | bytes 8388624 | tf_op jit(solution)/shard_map/broadcast_in_dim | solution.py:211
  385.6 0.2 convert_element_type.86
  385.9 32.5 %reduce-scatter.2.cloned.1.call-done = bf16[16,4096]{1,0:T(8,128)(2,1)} async-done(((bf16[128,4096]{1,0:T(8,128)(2,1)}), bf16[16,4096]{1,0:T(8,128)(2,1)}) %reduce-scatter.2.cloned.1.call-update) | async-done | bytes 131088 | tf_op jit(solution)/shard_map/reduce_scatter | solution.py:202
  418.3 1.6 add_convert_fusion.1
  (95 shorter events, 3.4 us)
Async XLA Ops:
  19.9 53.8 %all-to-all-start = ((bf16[16,2,128,512]{3,2,1,0:T(8,128)(2,1)}), bf16[16,2,128,512]{3,2,1,0:T(8,128)(2,1)}, u32[]{:S(2)}, u32[]{:S(2)}) async-start(bf16[16,2,128,512]{3,2,1,0:T(8,128)(2,1)} %broadcast_select_fusion.2), calls=%async_computation | async-start | bytes 8388608 | tf_op jit(solution)/shard_map/all_to_all | solution.py:70
  83.4 5.3 %copy-start.1 = (bf16[128,1024]{1,0:T(8,128)(2,1)S(1)}, bf16[128,1024]{1,0:T(8,128)(2,1)}, u32[]{:S(2)}) copy-start(bf16[128,1024]{1,0:T(8,128)(2,1)} %param.21) | copy-start | bytes 786436
  83.4 5.3 %copy-start.8 = (f32[1024]{0:T(1024)S(1)}, f32[1024]{0:T(1024)}, u32[]{:S(2)}) copy-start(f32[1024]{0:T(1024)} %param.22) | copy-start | bytes 12292
  83.4 97.9 %all-to-all-start.1 = ((bf16[16,2,128,512]{3,2,1,0:T(8,128)(2,1)}), bf16[16,2,128,512]{3,2,1,0:T(8,128)(2,1)}, u32[]{:S(2)}, u32[]{:S(2)}) async-start(bf16[16,2,128,512]{3,2,1,0:T(8,128)(2,1)} %broadcast_select_fusion.1), calls=%async_computation.1 | async-start | bytes 8388608 | tf_op jit(solution)/shard_map/all_to_all | solution.py:86
  88.6 4.2 copy-start.9
  88.6 4.2 copy-start.10
  88.6 4.5 %copy-start.5 = (bf16[128,2,512]{2,1,0:T(2,128)(2,1)S(1)}, bf16[128,2,512]{2,1,0:T(2,128)(2,1)}, u32[]{:S(2)}) copy-start(bf16[128,2,512]{2,1,0:T(2,128)(2,1)} %param.37) | copy-start | bytes 786436
  88.6 4.9 %copy-start.11 = (s32[1,16]{1,0:T(1,128)S(1)}, s32[1,16]{1,0:T(1,128)}, u32[]{:S(2)}) copy-start(s32[1,16]{1,0:T(1,128)} %param.36) | copy-start | bytes 196
  88.6 4.9 %copy-start.12 = (s32[1,8]{1,0:T(1,128)S(1)}, s32[1,8]{1,0:T(1,128)}, u32[]{:S(2)}) copy-start(s32[1,8]{1,0:T(1,128)} %param.32) | copy-start | bytes 100
  88.6 57.3 %all-reduce.4.cloned.1.call-start = ((), (), s32[]{:S(2)}) async-start(), calls=%async_computation.3 | async-start | bytes 2097152 | tf_op jit(solution)/shard_map/psum | solution.py:161
  92.7 176.0 %all-gather.3.cloned.1.call-start = ((), (), s32[]{:S(2)}) async-start(), calls=%async_computation.4 | async-start | bytes 5242880 | tf_op jit(solution)/shard_map/all_gather | solution.py:16
  186.3 2.9 copy-start.2
  202.0 0.7 copy-start.3
  218.5 116.9 %all-reduce.6.cloned.1.call-start = ((), (), s32[]{:S(2)}) async-start(), calls=%async_computation.5 | async-start | bytes 2097152 | tf_op jit(solution)/shard_map/psum | solution.py:191
  218.8 6.7 %copy-start.6 = (f32[24,4,4,128]{3,2,1,0:T(4,128)S(1)}, f32[24,4,4,128]{3,2,1,0:T(4,128)}, u32[]{:S(2)}) copy-start(f32[24,4,4,128]{3,2,1,0:T(4,128)} %get-tuple-element.261) | copy-start | bytes 589828
  218.8 15.4 %copy-start.4 = (f32[128,4,4]{2,1,0:T(4,128)S(1)}, f32[128,4,4]{2,1,0:T(4,128)}, u32[]{:S(2)}) copy-start(f32[128,4,4]{2,1,0:T(4,128)} %copy-done.3) | copy-start | bytes 24580
  280.6 77.9 %copy-start.7 = (f32[4096]{0:T(1024)S(1)}, f32[4096]{0:T(1024)}, u32[]{:S(2)}) copy-start(f32[4096]{0:T(1024)} %param.23) | copy-start | bytes 49156
  282.7 74.3 %all-reduce.8.cloned.1.call-start = ((), (), s32[]{:S(2)}) async-start(), calls=%async_computation.6 | async-start | bytes 2097152 | tf_op jit(solution)/shard_map/psum | solution.py:191
  335.3 83.0 %reduce-scatter.2.cloned.1.call-start = ((), (), s32[]{:S(2)}) async-start(), calls=%async_computation.7 | async-start | bytes 1179648 | tf_op jit(solution)/shard_map/reduce_scatter | solution.py:202
  358.5 7.7 %copy-start = (bf16[128,4096]{1,0:T(8,128)(2,1)S(1)}, bf16[128,4096]{1,0:T(8,128)(2,1)}, u32[]{:S(2)}) copy-start(bf16[128,4096]{1,0:T(8,128)(2,1)} %all-reduce.8.cloned.1.call-done) | copy-start | bytes 3145732
Sparse Core Ops, SparseCore 0:
  92.8 53.0 all-reduce.3
  218.6 50.0 all-gather.2
  282.8 52.4 all-reduce.5
  337.5 19.4 all-reduce.7
  381.1 37.1 reduce-scatter.1
